TPU v7x, 32 devices: a whole 2x2x4 slice. The times are simulated.
32 devices in a mesh: exp: 8 (over y, x, core), tp: 4 (over z).
Axes of the slice: x: 2, y: 2, z: 4, core: 2. Of those that a mesh axis runs over, the one named last changes fastest.
Arguments:
- tokens: bfloat16 [224, 4096], P('exp', 'tp'), may hold values from -6 to 6
- cotangent: bfloat16 [224, 4096], P('exp', 'tp'), may hold values from -6 to 6
- experts: int32 [224, 2], P('exp'), may hold values from 0 to 7, all different within a row; in each aligned block of 28 rows (0 to 27, 28 to 55, ...) at most 8 rows name the same one
- gates: float32 [224, 2], P('exp'), may hold values from 0.1 to 0.9
- w_gate: bfloat16 [8, 4096, 8192], P('exp', None, 'tp'), may hold values from -0.09375 to 0.09375
- w_up: bfloat16 [8, 4096, 8192], P('exp', None, 'tp'), may hold values from -0.09375 to 0.09375
- w_down: bfloat16 [8, 8192, 4096], P('exp', 'tp'), may hold values from -0.0625 to 0.0625
Outputs:
- output: bfloat16 [224, 4096], P('exp', 'tp')
- input_grad: bfloat16 [224, 4096], P('exp', 'tp')
- grad_gate: bfloat16 [8, 4096, 8192], P('exp', None, 'tp')
- grad_up: bfloat16 [8, 4096, 8192], P('exp', None, 'tp')
- grad_down: bfloat16 [8, 8192, 4096], P('exp', 'tp')
Inputs may be any that keep to these rules, and one draw needn't show every extreme that they name: Each row names 2 different experts. In each aligned block of 28 rows (the rows of one index of exp) no expert is named by more than 8 rows, and in some blocks one is named by exactly 8.
All inputs are finite; a program needn't handle non-finite values.
Results may differ from a plain program's by a relative error of at most 0.017.
Values may be sent and summed in bfloat16 or wider, within the bound.
A program may use at most 192 MiB of HBM per device.

v0:
```python
import functools

import jax
import jax.numpy as jnp
from jax import lax
from jax.experimental import pallas as pl
from jax.experimental.pallas import tpu as pltpu
from jax.sharding import PartitionSpec as P

EXPERTS = 8
CAP = 8
MESH = pl.DeviceIdType.MESH


def contract_rows(left, right):
    return lax.dot_general(
        left, right, (((0,), (0,)), ((), ())), preferred_element_type=jnp.float32
    )


def contract_cols(left, right):
    return lax.dot_general(
        left, right, (((1,), (1,)), ((), ())), preferred_element_type=jnp.float32
    )


def slot_places(experts, capacity):
    pair_ids = experts.reshape(-1)
    matches = (pair_ids[:, None] == jnp.arange(EXPERTS, dtype=jnp.int32)[None, :]).astype(jnp.int32)
    before = jnp.cumsum(matches, axis=0) - matches
    slot_ids = jnp.sum(before * matches, axis=1)
    return pair_ids * capacity + slot_ids


def forward_kernel(n, m, group, bf, depth, send_ref, wg_hbm, wu_hbm, wd_hbm, *rest):
    x_ref, g_ref, a_ref, d1_ref, d3_ref = rest[:5]
    parts = rest[5 : 5 + m]
    (wg, wu, wd, w_sem, held, y_acc, b_acc, s1, r1, s2, r2) = rest[5 + m :]
    e, t = lax.axis_index("exp"), lax.axis_index("tp")
    cols = send_ref.shape[2]
    blocks = wg_hbm.shape[2] // bf

    def weight_copies(j, slot):
        span = pl.ds(pl.multiple_of(j * bf, bf), bf)
        return (
            pltpu.make_async_copy(wg_hbm.at[0, :, span], wg.at[slot], w_sem.at[slot, 0]),
            pltpu.make_async_copy(wu_hbm.at[0, :, span], wu.at[slot], w_sem.at[slot, 1]),
            pltpu.make_async_copy(wd_hbm.at[0, span, :], wd.at[slot], w_sem.at[slot, 2]),
        )

    barrier = pltpu.get_barrier_semaphore()
    for r in range(1, n):
        pl.semaphore_signal(
            barrier, inc=1, device_id={"exp": lax.rem(e + r, n), "tp": t}, device_id_type=MESH
        )
    for q in range(1, m):
        pl.semaphore_signal(
            barrier, inc=1, device_id={"exp": e, "tp": lax.rem(t + q, m)}, device_id_type=MESH
        )
    for j in range(depth):
        for copy in weight_copies(j, j):
            copy.start()
    pl.semaphore_wait(barrier, n - 1 + m - 1)

    def rows_of(source):
        return pl.ds(pl.multiple_of(source * 2 * CAP, 2 * CAP), 2 * CAP)

    def cols_of(part):
        return pl.ds(pl.multiple_of(part * cols, cols), cols)

    first = []
    for r in range(1, n):
        dest = lax.rem(e + r, n)
        copy = pltpu.make_async_remote_copy(
            src_ref=send_ref.at[dest // group],
            dst_ref=held.at[rows_of(e), cols_of(t)],
            send_sem=s1.at[r],
            recv_sem=r1.at[r],
            device_id={"exp": dest, "tp": t},
            device_id_type=MESH,
        )
        copy.start()
        first.append(copy)
    second = []
    for r in range(n):
        source = lax.rem(e - r + n, n)
        here = held.at[rows_of(source), cols_of(t)]
        if r > 0:
            first[r - 1].wait_recv()
        for q in range(1, m):
            copy = pltpu.make_async_remote_copy(
                src_ref=here if r > 0 else send_ref.at[e // group],
                dst_ref=here,
                send_sem=s2.at[r, q],
                recv_sem=r2.at[r, q],
                device_id={"exp": e, "tp": lax.rem(t + q, m)},
                device_id_type=MESH,
            )
            copy.start()
            second.append(copy)
    held[rows_of(e), cols_of(t)] = send_ref[e // group]
    y_acc[...] = jnp.zeros_like(y_acc)
    b_acc[...] = jnp.zeros_like(b_acc)
    for copy in second:
        copy.wait_recv()
    for part in range(m):
        span = pl.ds(part * cols, cols)
        pair = held[:, span].astype(jnp.float32).reshape(n, 2, CAP, cols)
        x_ref[:, span] = pair[:, 0].reshape(n * CAP, cols).astype(jnp.bfloat16)
        g_ref[:, span] = pair[:, 1].reshape(n * CAP, cols).astype(jnp.bfloat16)

    @pl.loop(0, blocks)
    def _(j):
        slot = lax.rem(j, depth)
        for copy in weight_copies(j, slot):
            copy.wait()
        span = pl.ds(pl.multiple_of(j * bf, bf), bf)
        h1 = jnp.dot(x_ref[...], wg[slot], preferred_element_type=jnp.float32)
        h3 = jnp.dot(x_ref[...], wu[slot], preferred_element_type=jnp.float32)
        da = contract_cols(g_ref[...], wd[slot])
        sig = jax.nn.sigmoid(h1)
        act = (h1 * sig * h3).astype(jnp.bfloat16)
        d1 = (da * h3 * sig * (1.0 + h1 * (1.0 - sig))).astype(jnp.bfloat16)
        d3 = (da * h1 * sig).astype(jnp.bfloat16)
        a_ref[:, span] = act
        d1_ref[:, span] = d1
        d3_ref[:, span] = d3
        y_acc[...] += jnp.dot(act, wd[slot], preferred_element_type=jnp.float32)
        b_acc[...] += contract_cols(d1, wg[slot]) + contract_cols(d3, wu[slot])

        @pl.when(j + depth < blocks)
        def _():
            for copy in weight_copies(j + depth, slot):
                copy.start()

    for r in range(m):
        span = cols_of(lax.rem(t + r, m))
        parts[r][0] = y_acc[:, span].astype(jnp.bfloat16)
        parts[r][1] = b_acc[:, span].astype(jnp.bfloat16)
    for copy in first + second:
        copy.wait_send()


def wide_kernel(x_ref, d1_ref, d3_ref, gate_ref, up_ref, xt):
    @pl.when(pl.program_id(0) == 0)
    def _():
        xt[...] = x_ref[...].astype(jnp.float32).T.astype(jnp.bfloat16)

    gate_ref[0] = jnp.dot(xt[...], d1_ref[...], preferred_element_type=jnp.float32).astype(
        jnp.bfloat16
    )
    up_ref[0] = jnp.dot(xt[...], d3_ref[...], preferred_element_type=jnp.float32).astype(
        jnp.bfloat16
    )


def sum_kernel(_, *rest):
    parts, out_ref = rest[:-1], rest[-1]
    total = parts[0][...].astype(jnp.float32)
    for part in parts[1:]:
        total = total + part[...].astype(jnp.float32)
    n, _, cap, cols = out_ref.shape
    for which in range(2):
        out_ref[:, which] = total[which].reshape(n, cap, cols).astype(out_ref.dtype)


def down_kernel(_, a_ref, g_ref, down_ref):
    down_ref[0] = contract_rows(a_ref[...], g_ref[...]).astype(jnp.bfloat16)


def per_device(tokens, cotangent, experts, gates, w_gate, w_up, w_down):
    n, m = lax.axis_size("exp"), lax.axis_size("tp")
    group = n // EXPERTS
    tok_rows, top_count = experts.shape
    width, hidden = w_gate.shape[1], w_gate.shape[2]
    cols = tokens.shape[1]
    rows = n * CAP
    bf = min(256, hidden)
    blocks = hidden // bf
    depth = min(6, blocks)

    places = slot_places(experts, CAP)
    pick = (
        places[:, None] == jnp.arange(EXPERTS * CAP, dtype=jnp.int32)[None, :]
    ).astype(jnp.float32)
    per_token = pick.reshape(tok_rows, top_count, EXPERTS * CAP)
    weighted = jnp.sum(per_token * gates[:, :, None], axis=1)
    unweighted = jnp.sum(per_token, axis=1)
    row_gate = jnp.sum(weighted, axis=0)
    pick_low = unweighted.astype(jnp.bfloat16)
    both = jnp.concatenate([tokens, cotangent], axis=1)
    picked = contract_rows(pick_low, both)
    token_rows = picked[:, :cols].astype(jnp.bfloat16)
    scaled = (picked[:, cols:] * row_gate[:, None]).astype(jnp.bfloat16)
    send = jnp.concatenate(
        [token_rows.reshape(EXPERTS, CAP, cols), scaled.reshape(EXPERTS, CAP, cols)], axis=1
    )

    vmem = pl.BlockSpec(memory_space=pltpu.VMEM)
    anyw = pl.BlockSpec(memory_space=pl.ANY)
    low = jnp.bfloat16
    wide = jax.ShapeDtypeStruct((rows, width), low)
    narrow = jax.ShapeDtypeStruct((rows, hidden), low)
    part = jax.ShapeDtypeStruct((2, rows, cols), low)
    outs = pl.pallas_call(
        functools.partial(forward_kernel, n, m, group, bf, depth),
        out_shape=[wide, wide, narrow, narrow, narrow] + [part] * m,
        in_specs=[vmem, anyw, anyw, anyw],
        out_specs=[vmem] * (5 + m),
        scratch_shapes=[
            pltpu.VMEM((depth, width, bf), low),
            pltpu.VMEM((depth, width, bf), low),
            pltpu.VMEM((depth, bf, width), low),
            pltpu.SemaphoreType.DMA((depth, 3)),
            pltpu.VMEM((2 * rows, width), low),
            pltpu.VMEM((rows, width), jnp.float32),
            pltpu.VMEM((rows, width), jnp.float32),
            pltpu.SemaphoreType.DMA((n,)),
            pltpu.SemaphoreType.DMA((n,)),
            pltpu.SemaphoreType.DMA((n, m)),
            pltpu.SemaphoreType.DMA((n, m)),
        ],
        compiler_params=pltpu.CompilerParams(
            collective_id=0, has_side_effects=True, vmem_limit_bytes=60 * 1024 * 1024
        ),
        cost_estimate=pl.CostEstimate(
            flops=12 * rows * width * hidden,
            bytes_accessed=6 * width * hidden,
            transcendentals=rows * hidden,
        ),
        name="forward",
    )(send, w_gate, w_up, w_down)
    x, g, act, d1, d3 = outs[:5]
    parts = outs[5:]

    got = [
        lax.ppermute(parts[r], "tp", [(i, (i + r) % m) for i in range(m)]) for r in range(1, m)
    ]

    gb = min(256, hidden)
    full = pl.BlockSpec((rows, width), lambda j: (0, 0))
    strip = pl.BlockSpec((rows, gb), lambda j: (0, j))
    grad_gate, grad_up = pl.pallas_call(
        wide_kernel,
        out_shape=[jax.ShapeDtypeStruct(w_gate.shape, low)] * 2,
        grid=(hidden // gb,),
        in_specs=[full, strip, strip],
        out_specs=[pl.BlockSpec((1, width, gb), lambda j: (0, 0, j))] * 2,
        scratch_shapes=[pltpu.VMEM((width, rows), low)],
        compiler_params=pltpu.CompilerParams(
            dimension_semantics=("arbitrary",), vmem_limit_bytes=40 * 1024 * 1024
        ),
        cost_estimate=pl.CostEstimate(
            flops=4 * rows * width * hidden, bytes_accessed=4 * width * hidden, transcendentals=0
        ),
        name="grad_wide",
    )(x, d1, d3)
    total = pl.pallas_call(
        sum_kernel,
        out_shape=jax.ShapeDtypeStruct((n, 2, CAP, cols), low),
        in_specs=[anyw] + [vmem] * m,
        out_specs=vmem,
        name="sum_parts",
    )(grad_gate, parts[0], *got)
    grad_down = pl.pallas_call(
        down_kernel,
        out_shape=jax.ShapeDtypeStruct(w_down.shape, low),
        grid=(hidden // gb,),
        in_specs=[anyw, strip, full],
        out_specs=pl.BlockSpec((1, gb, width), lambda j: (0, j, 0)),
        compiler_params=pltpu.CompilerParams(
            dimension_semantics=("arbitrary",), vmem_limit_bytes=40 * 1024 * 1024
        ),
        cost_estimate=pl.CostEstimate(
            flops=2 * rows * width * hidden, bytes_accessed=2 * width * hidden, transcendentals=0
        ),
        name="grad_down",
    )(total, act, g)

    back = lax.all_to_all(total, "exp", split_axis=0, concat_axis=0, tiled=True)
    back = back.astype(jnp.float32).reshape(EXPERTS, group, 2, CAP, cols)
    back = jnp.sum(back, axis=1).transpose(1, 0, 2, 3).reshape(2, EXPERTS * CAP, cols)

    def combine(table, values):
        return jnp.dot(
            table, values, precision=lax.Precision.HIGHEST, preferred_element_type=jnp.float32
        ).astype(low)

    return (
        combine(weighted, back[0]),
        combine(unweighted, back[1]),
        grad_gate,
        grad_up,
        grad_down,
    )


def solution(mesh):
    in_specs = (
        P("exp", "tp"),
        P("exp", "tp"),
        P("exp", None),
        P("exp", None),
        P("exp", None, "tp"),
        P("exp", None, "tp"),
        P("exp", "tp", None),
    )
    out_specs = (
        P("exp", "tp"),
        P("exp", "tp"),
        P("exp", None, "tp"),
        P("exp", None, "tp"),
        P("exp", "tp", None),
    )
    return jax.shard_map(
        per_device, mesh=mesh, in_specs=in_specs, out_specs=out_specs, check_vma=False
    )
```

profile of v0, /device:TPU:11, one launch (start us, length us, event | category | flops | bytes accessed | tf_op | source)
XLA Modules:
  0.0 110.0 jit_solution(16387179436777074670)
XLA Ops:
  0.6 0.8 copy.24
  1.4 0.1 eq.29
  1.5 0.1 fusion.7
  1.6 0.1 reduce_window_sum.11
  1.7 0.2 select_reduce_fusion.2
  1.9 0.1 reduce_sum.43
  2.0 0.1 copy.25
  2.1 0.7 multiply_add_fusion
  2.7 0.1 copy.26
  2.8 0.8 copy.27
  3.6 0.2 select_reduce_fusion
  3.8 1.1 %fusion.3 = f32[64,2048]{1,0:T(8,128)S(1)} fusion(bf16[28,1024]{1,0:T(8,128)(2,1)} %param.8, bf16[28,1024]{1,0:T(8,128)(2,1)} %param.7, f32[28,64]{1,0:T(8,128)S(1)} %get-tuple-element.29), kind=kOutput, calls=%fused_computation.10 | convolution fusion | flops 7571200 | bytes 646144 | tf_op jit(solution)/shard_map/dot_general | solution.py:16
  4.9 0.1 fusion.2
  5.0 0.7 pad_maximum_fusion.send_ref
  5.7 58.6 %forward.1 = (bf16[64,4096]{1,0:T(8,128)(2,1)}, bf16[64,4096]{1,0:T(8,128)(2,1)}, bf16[64,2048]{1,0:T(8,128)(2,1)}, bf16[64,2048]{1,0:T(8,128)(2,1)}, bf16[64,20...) custom-call(bf16[8,16,1024]{2,1,0:T(8,128)(2,1)} %pad_maximum_fusion, ...), custom_call_target="tpu_custom_call" | custom-call | flops 6442450944 | bytes 50331648 | tf_op jit(solution)/shard_map/forward/pallas_call | solution.py:205
  64.3 0.0 copy-start.1
  64.3 0.0 copy-start.2
  64.3 0.1 collective-permute-start
  64.4 2.5 %collective-permute-start.1 = (bf16[2,64,1024]{2,1,0:T(8,128)(2,1)}, bf16[2,64,1024]{2,1,0:T(8,128)(2,1)S(1)}, u32[]{:S(2)}, u32[]{:S(2)}) collective-permute-start(bf16[2,64,1024]{2,1,0:T(8,128)(2,1)} %get-tuple-element.22), channel_id=1, source_target_pairs={{0,2},{1,3},{2,0},{3,1},{4,6},{5,7},{6,4},{7,5},{8,10},{9,11},{10,... | collective-permute-start | bytes 786440 | tf_op jit(solution)/shard_map/ppermute | solution.py:237
  66.9 0.4 collective-permute-start.2
  67.4 0.0 copy-start.3
  67.4 1.0 copy-done.3
  68.4 0.0 copy-start.4
  68.4 0.9 copy-done.4
  69.4 0.0 copy-start.5
  69.4 0.9 copy-done.5
  70.3 14.5 %grad_wide.1 = (bf16[1,4096,2048]{2,1,0:T(8,128)(2,1)}, bf16[1,4096,2048]{2,1,0:T(8,128)(2,1)}) custom-call(bf16[64,4096]{1,0:T(8,128)(2,1)S(1)} %copy-done.3, bf16[64,2048]{1,0:T(8,128)(2,1)S(1)} %copy-done.4, bf16[64,2048]{1,0:T(8,128)(2,1)S(1)} %copy-done.5), custom_call_target="tpu_custom_call" | custom-call | flops 2147483648 | bytes 33554432 | tf_op jit(solution)/shard_map/grad_wide/pallas_call | solution.py:243
  84.8 0.0 collective-permute-done.rest_1_
  84.8 0.0 copy-start.6
  84.8 1.0 collective-permute-done.1.rest_2_
  85.8 0.0 copy-start.7
  85.8 5.0 %collective-permute-done.2.rest_3_ = bf16[2,64,1024]{2,1,0:T(8,128)(2,1)S(1)} collective-permute-done((bf16[2,64,1024]{2,1,0:T(8,128)(2,1)}, bf16[2,64,1024]{2,1,0:T(8,128)(2,1)S(1)}, u32[]{:S(2)}, u32[]{:S(2)}) %collective-permute-start.2) | collective-permute-done | bytes 262176 | tf_op jit(solution)/shard_map/ppermute | solution.py:237
  90.8 0.0 copy-start.8
  90.8 0.0 copy-done.6
  90.8 0.0 copy-done.7
  90.8 0.7 copy-done.8
  91.5 2.0 %sum_parts.1._ = bf16[8,2,8,1024]{3,2,1,0:T(8,128)(2,1)} custom-call(bf16[1,4096,2048]{2,1,0:T(8,128)(2,1)} %get-tuple-element.13._, bf16[2,64,1024]{2,1,0:T(8,128)(2,1)} %get-tuple-element.20.rest_0_, bf16[2,64,1024]{2,1,0:T(8,128)(2,1)} %copy-done.6, bf16[2,64,1024]{2,1,0:T(8,128)(2,1)} %copy-done.7, bf16[2,64,1024]{2,1,0:T(8,128)(2,1)} %copy-done.8), custom_call_target="tpu_custom_call" | custom-call | tf_op jit(solution)/shard_map/sum_parts/pallas_call | solution.py:258
  93.5 4.9 %all-to-all-start = ((bf16[8,2,8,1024]{3,2,1,0:T(8,128)(2,1)}), bf16[8,2,8,1024]{3,2,1,0:T(8,128)(2,1)S(1)}, u32[]{:S(2)}, u32[]{:S(2)}) async-start(bf16[8,2,8,1024]{3,2,1,0:T(8,128)(2,1)} %sum_parts.1._), calls=%async_computation | async-start | bytes 524288 | tf_op jit(solution)/shard_map/all_to_all | solution.py:280
  98.4 0.0 copy-done.1
  98.4 0.0 copy-done.2
  98.4 0.0 copy-start
  98.4 1.0 copy-done
  99.4 9.0 %grad_down.1 = bf16[1,2048,4096]{2,1,0:T(8,128)(2,1)} custom-call(bf16[8,2,8,1024]{3,2,1,0:T(8,128)(2,1)S(1)} %copy-done, bf16[64,2048]{1,0:T(8,128)(2,1)S(1)} %copy-done.2, bf16[64,4096]{1,0:T(8,128)(2,1)S(1)} %copy-done.1), custom_call_target="tpu_custom_call" | custom-call | flops 1073741824 | bytes 16777216 | tf_op jit(solution)/shard_map/grad_down/pallas_call | solution.py:265
  108.3 0.0 all-to-all-done
  108.3 0.8 convolution_convert_fusion
  109.2 0.8 convolution_convert_fusion.1
  (1 shorter events, 0.0 us)
Async XLA Ops:
  64.3 34.1 %copy-start.1 = (bf16[64,4096]{1,0:T(8,128)(2,1)S(1)}, bf16[64,4096]{1,0:T(8,128)(2,1)}, u32[]{:S(2)}) copy-start(bf16[64,4096]{1,0:T(8,128)(2,1)} %get-tuple-element.26.g_ref) | copy-start | bytes 1572868
  64.3 34.1 %copy-start.2 = (bf16[64,2048]{1,0:T(8,128)(2,1)S(1)}, bf16[64,2048]{1,0:T(8,128)(2,1)}, u32[]{:S(2)}) copy-start(bf16[64,2048]{1,0:T(8,128)(2,1)} %get-tuple-element.25.a_ref) | copy-start | bytes 786436
  64.3 20.5 %collective-permute-start = (bf16[2,64,1024]{2,1,0:T(8,128)(2,1)}, bf16[2,64,1024]{2,1,0:T(8,128)(2,1)S(1)}, u32[]{:S(2)}, u32[]{:S(2)}) collective-permute-start(bf16[2,64,1024]{2,1,0:T(8,128)(2,1)} %get-tuple-element.21), channel_id=1, source_target_pairs={{0,1},{1,2},{2,3},{3,0},{4,5},{5,6},{6,7},{7,4},{8,9},{9,10},{10,1... | collective-permute-start | bytes 786440 | tf_op jit(solution)/shard_map/ppermute | solution.py:237
  64.4 21.4 %collective-permute-start.1 = (bf16[2,64,1024]{2,1,0:T(8,128)(2,1)}, bf16[2,64,1024]{2,1,0:T(8,128)(2,1)S(1)}, u32[]{:S(2)}, u32[]{:S(2)}) collective-permute-start(bf16[2,64,1024]{2,1,0:T(8,128)(2,1)} %get-tuple-element.22), channel_id=1, source_target_pairs={{0,2},{1,3},{2,0},{3,1},{4,6},{5,7},{6,4},{7,5},{8,10},{9,11},{10,... | collective-permute-start | bytes 786440 | tf_op jit(solution)/shard_map/ppermute | solution.py:237
  66.9 23.9 %collective-permute-start.2 = (bf16[2,64,1024]{2,1,0:T(8,128)(2,1)}, bf16[2,64,1024]{2,1,0:T(8,128)(2,1)S(1)}, u32[]{:S(2)}, u32[]{:S(2)}) collective-permute-start(bf16[2,64,1024]{2,1,0:T(8,128)(2,1)} %get-tuple-element.23), channel_id=1, source_target_pairs={{0,3},{1,0},{2,1},{3,2},{4,7},{5,4},{6,5},{7,6},{8,11},{9,8},{10,9... | collective-permute-start | bytes 786440 | tf_op jit(solution)/shard_map/ppermute | solution.py:237
  67.4 1.0 copy-start.3
  68.4 0.9 copy-start.4
  69.4 0.9 copy-start.5
  84.8 6.0 %copy-start.6 = (bf16[2,64,1024]{2,1,0:T(8,128)(2,1)}, bf16[2,64,1024]{2,1,0:T(8,128)(2,1)S(1)}, u32[]{:S(2)}) copy-start(bf16[2,64,1024]{2,1,0:T(8,128)(2,1)S(1)} %collective-permute-done.rest_1_) | copy-start | bytes 786436
  85.8 5.0 %copy-start.7 = (bf16[2,64,1024]{2,1,0:T(8,128)(2,1)}, bf16[2,64,1024]{2,1,0:T(8,128)(2,1)S(1)}, u32[]{:S(2)}) copy-start(bf16[2,64,1024]{2,1,0:T(8,128)(2,1)S(1)} %collective-permute-done.1.rest_2_) | copy-start | bytes 786436
  90.8 0.7 copy-start.8
  93.5 14.8 %all-to-all-start = ((bf16[8,2,8,1024]{3,2,1,0:T(8,128)(2,1)}), bf16[8,2,8,1024]{3,2,1,0:T(8,128)(2,1)S(1)}, u32[]{:S(2)}, u32[]{:S(2)}) async-start(bf16[8,2,8,1024]{3,2,1,0:T(8,128)(2,1)} %sum_parts.1._), calls=%async_computation | async-start | bytes 524288 | tf_op jit(solution)/shard_map/all_to_all | solution.py:280
  98.4 1.0 copy-start
where the time goes:
time: 110 us
  Pallas kernels  84 us (76%)
  starting transfers between devices  7.88 us (7%)
  local copies, waits for them, and re-layouts  6.57 us (6%)
  waiting for transfers between devices  6.01 us (5%)
  matrix products  2.77 us (3%)
  other arithmetic  2 us (2%)
    pallas_call x1, Pallas kernels, per_device(): pl.pallas_call(functools.partial(forward_kernel, n, m, group, bf, depth),...  58.6 us
    pallas_call x1, Pallas kernels, per_device(): pl.pallas_call(wide_kernel, out_shape=[jax.ShapeDtypeStruct(w_gate.shape,...  14.5 us
    pallas_call x1, Pallas kernels, per_device(): pl.pallas_call(down_kernel, out_shape=jax.ShapeDtypeStruct(w_down.shape,...  8.96 us
    unnamed x20, local copies, waits for them, and re-layouts  6.16 us
    ppermute x3, waiting for transfers between devices, per_device(): lax.ppermute(parts[r], 'tp', [(i, (i + r) % m) for i in range(m)])  6.01 us
    all_to_all x1, starting transfers between devices, per_device(): back = lax.all_to_all(total, 'exp', split_axis=0, concat_axis=0, tiled=True)  4.85 us
    ppermute x3, starting transfers between devices, per_device(): lax.ppermute(parts[r], 'tp', [(i, (i + r) % m) for i in range(m)])  3.02 us
  transfers between devices with their start and end apart: 4, of which 2 were waited for; matrix products, arithmetic and copies ran while one was open for 0% of the time, Pallas kernels for 21%

commit v1 on v0

v1 whole, which is shorter than its diff:
```python
import functools

import jax
import jax.numpy as jnp
from jax import lax
from jax.experimental import pallas as pl
from jax.experimental.pallas import tpu as pltpu
from jax.sharding import PartitionSpec as P

EXPERTS = 8
CAP = 8
PAIR = 2 * CAP
MESH = pl.DeviceIdType.MESH
LOW = jnp.bfloat16
F32 = jnp.float32


def contract_rows(left, right):
    return lax.dot_general(left, right, (((0,), (0,)), ((), ())), preferred_element_type=F32)


def contract_cols(left, right):
    return lax.dot_general(left, right, (((1,), (1,)), ((), ())), preferred_element_type=F32)


def flip(index, bits):
    out, unit = index, 1
    while unit <= bits:
        if bits & unit:
            out = out + unit * (1 - 2 * ((index // unit) % 2))
        unit *= 2
    return out


def round_up(value, unit):
    return -(-value // unit) * unit


def make_tables(group, experts_ref, gates_ref, table, pick, comb):
    count = experts_ref.shape[0]
    pad = round_up(count, 16)
    lane = lax.broadcasted_iota(jnp.int32, (count, 128), 1)
    ids = [experts_ref[:, j : j + 1] for j in range(2)]
    gates = [gates_ref[:, j : j + 1] for j in range(2)]
    hits = [(ids[j] == lane).astype(F32) for j in range(2)]
    tri = (
        lax.broadcasted_iota(jnp.int32, (count, count), 0)
        > lax.broadcasted_iota(jnp.int32, (count, count), 1)
    ).astype(F32)
    before = jnp.dot(tri, hits[0] + hits[1], preferred_element_type=F32)
    places = [
        ids[j] * CAP + jnp.sum(before * hits[j], axis=1, keepdims=True).astype(jnp.int32)
        for j in range(2)
    ]
    table[...] = jnp.zeros_like(table)
    comb[...] = jnp.zeros_like(comb)

    def columns(width, share):
        col = lax.broadcasted_iota(jnp.int32, (count, width), 1)
        owner = col // (PAIR * share)
        return owner * CAP + col % CAP, (col % PAIR) < CAP

    where, first = columns(EXPERTS * PAIR, 1)
    hit = [places[j] == where for j in range(2)]
    table[0:count, :] = ((hit[0] | hit[1]) & first).astype(F32)
    for j in range(2):
        table[(1 + j) * pad : (1 + j) * pad + count, :] = jnp.where(first, 0.0, hit[j].astype(F32))
    pick[...] = table[...].T.astype(LOW)

    where, first = columns(comb.shape[1], group)
    hit = [(places[j] == where).astype(F32) for j in range(2)]
    weight = jnp.where(first, hit[0] * gates[0] + hit[1] * gates[1], 0.0)
    for part in range(3):
        piece = weight.astype(LOW)
        comb[part * pad : part * pad + count, :] = piece
        weight = weight - piece.astype(F32)
    comb[3 * pad : 3 * pad + count, :] = jnp.where(first, 0.0, hit[0] + hit[1]).astype(LOW)


def forward_kernel(
    n, m, group, bf, bc,
    tok_hbm, cot_hbm, experts_ref, gates_ref, wg_hbm, wu_hbm, wd_hbm,
    x_ref, g_ref, a_ref, d1_ref, d3_ref, out_ref,
    wg, wu, wd, w_sem, tok, t_sem, table, pick, comb, stack, send, held,
    h1_acc, h3_acc, da_acc, back, home, part_send, got,
    sa, ra, sb, rb, sc, rc, sd, rd,
):
    e, t = lax.axis_index("exp"), lax.axis_index("tp")
    count, cols = tok_hbm.shape
    hidden = wg.shape[1]
    pad = round_up(count, 16)
    parts = [flip(t, q) for q in range(m)]

    def cols_of(q):
        return pl.ds(pl.multiple_of(parts[q] * cols, cols), cols)

    def rows_of(device):
        return pl.ds(pl.multiple_of(device * PAIR, PAIR), PAIR)

    own = [
        pltpu.make_async_copy(src, tok.at[0, i], t_sem.at[i])
        for i, src in enumerate((tok_hbm, cot_hbm))
    ]
    for copy in own:
        copy.start()
    barrier = pltpu.get_barrier_semaphore()
    for r in range(1, n):
        pl.semaphore_signal(
            barrier, inc=1, device_id={"exp": lax.rem(e + r, n), "tp": t}, device_id_type=MESH
        )
    for q in range(1, m):
        pl.semaphore_signal(
            barrier, inc=1, device_id={"exp": e, "tp": parts[q]}, device_id_type=MESH
        )
    loads = []
    for q in range(m):
        span = cols_of(q)
        loads.append((
            pltpu.make_async_copy(wg_hbm.at[0, span, :], wg.at[span, :], w_sem.at[q, 0]),
            pltpu.make_async_copy(wu_hbm.at[0, span, :], wu.at[span, :], w_sem.at[q, 1]),
            pltpu.make_async_copy(wd_hbm.at[0, :, span], wd.at[:, span], w_sem.at[q, 2]),
        ))
        for copy in loads[q]:
            copy.start()
    make_tables(group, experts_ref, gates_ref, table, pick, comb)
    stack[...] = jnp.zeros_like(stack)
    for copy in own:
        copy.wait()
    pl.semaphore_wait(barrier, n - 1 + m - 1)

    gather = [None]
    for q in range(1, m):
        gather.append(
            pltpu.make_async_remote_copy(
                src_ref=tok.at[0],
                dst_ref=tok.at[q],
                send_sem=sa.at[q],
                recv_sem=ra.at[q],
                device_id={"exp": e, "tp": parts[q]},
                device_id_type=MESH,
            )
        )
        gather[q].start()

    def to_experts(q, r):
        dest = lax.rem(e + r, n)
        return pltpu.make_async_remote_copy(
            src_ref=send.at[dest // group, :, cols_of(q)],
            dst_ref=held.at[rows_of(e), cols_of(q)],
            send_sem=sb.at[q, r],
            recv_sem=rb.at[q, r],
            device_id={"exp": dest, "tp": t},
            device_id_type=MESH,
        )

    def to_tokens(q, r):
        dest = lax.rem(e + r, n)
        return pltpu.make_async_remote_copy(
            src_ref=back.at[rows_of(dest), cols_of(q)],
            dst_ref=home.at[rows_of(e), cols_of(q)],
            send_sem=sc.at[q, r],
            recv_sem=rc.at[q, r],
            device_id={"exp": dest, "tp": t},
            device_id_type=MESH,
        )

    def to_owner(q):
        return pltpu.make_async_remote_copy(
            src_ref=part_send.at[q],
            dst_ref=got.at[q],
            send_sem=sd.at[q],
            recv_sem=rd.at[q],
            device_id={"exp": e, "tp": parts[q]},
            device_id_type=MESH,
        )

    def dispatch(q):
        if q > 0:
            gather[q].wait_recv()
        stack[0:count, :] = tok[q, 0]
        cot = tok[q, 1].astype(F32)
        for j in range(2):
            stack[(1 + j) * pad : (1 + j) * pad + count, :] = (
                cot * gates_ref[:, j : j + 1]
            ).astype(LOW)
        rows = jnp.dot(pick[...], stack[...], preferred_element_type=F32).astype(LOW)
        send[:, :, cols_of(q)] = rows.reshape(EXPERTS, PAIR, cols)

        @pl.loop(1, n)
        def _(r):
            to_experts(q, r).start()

        held[rows_of(e), cols_of(q)] = send[e // group, :, cols_of(q)]

    def phase_one(q):
        span = cols_of(q)

        @pl.loop(1, n)
        def _(r):
            to_experts(q, r).wait_recv()

        pair = held[:, span].astype(F32).reshape(n, 2, CAP, cols)
        x_ref[:, span] = pair[:, 0].reshape(n * CAP, cols).astype(LOW)
        g_ref[:, span] = pair[:, 1].reshape(n * CAP, cols).astype(LOW)
        for copy in loads[q]:
            copy.wait()

        @pl.loop(0, hidden // bf)
        def _(j):
            units = pl.ds(pl.multiple_of(j * bf, bf), bf)
            x, g = x_ref[:, span], g_ref[:, span]
            h1 = jnp.dot(x, wg[span, units], preferred_element_type=F32)
            h3 = jnp.dot(x, wu[span, units], preferred_element_type=F32)
            da = contract_cols(g, wd[units, span])
            if q == 0:
                h1_acc[:, units] = h1
                h3_acc[:, units] = h3
                da_acc[:, units] = da
            else:
                h1_acc[:, units] += h1
                h3_acc[:, units] += h3
                da_acc[:, units] += da

    def phase_two(q):
        @pl.loop(0, cols // bc)
        def _(j):
            span = pl.ds(pl.multiple_of(parts[q] * cols + j * bc, bc), bc)
            y = jnp.dot(a_ref[...], wd[:, span], preferred_element_type=F32)
            b = contract_cols(d1_ref[...], wg[span, :]) + contract_cols(d3_ref[...], wu[span, :])
            both = jnp.concatenate([y.reshape(n, CAP, bc), b.reshape(n, CAP, bc)], axis=1)
            back[:, span] = both.reshape(n * PAIR, bc).astype(LOW)

        @pl.loop(1, n)
        def _(r):
            to_tokens(q, r).start()

        home[rows_of(e), cols_of(q)] = back[rows_of(e), cols_of(q)]

    def combine(q):
        @pl.loop(1, n)
        def _(r):
            to_tokens(q, r).wait_recv()

        made = jnp.dot(comb[...], home[:, cols_of(q)], preferred_element_type=F32)
        output = made[0:pad] + made[pad : 2 * pad] + made[2 * pad : 3 * pad]
        return output[0:count], made[3 * pad : 3 * pad + count]

    def reduce(q):
        output, grad = combine(q)
        part_send[q, 0] = output.astype(LOW)
        part_send[q, 1] = grad.astype(LOW)
        to_owner(q).start()

    dispatch(0)
    for q in range(1, m):
        dispatch(q)
        phase_one(q - 1)
    phase_one(m - 1)

    @pl.loop(0, hidden // bf)
    def _(j):
        units = pl.ds(pl.multiple_of(j * bf, bf), bf)
        h1, h3, da = h1_acc[:, units], h3_acc[:, units], da_acc[:, units]
        sig = jax.nn.sigmoid(h1)
        a_ref[:, units] = (h1 * sig * h3).astype(LOW)
        d1_ref[:, units] = (da * h3 * sig * (1.0 + h1 * (1.0 - sig))).astype(LOW)
        d3_ref[:, units] = (da * h1 * sig).astype(LOW)

    for q in reversed(range(m)):
        phase_two(q)
        if q + 1 < m:
            reduce(q + 1)
    totals = list(combine(0))
    for q in range(1, m):
        to_owner(q).wait_recv()
        for i in range(2):
            totals[i] = totals[i] + got[q, i].astype(F32)
    for i in range(2):
        out_ref[i] = totals[i].astype(LOW)

    for q in range(1, m):
        gather[q].wait_send()
        to_owner(q).wait_send()
    for q in range(m):
        @pl.loop(1, n)
        def _(r):
            to_experts(q, r).wait_send()
            to_tokens(q, r).wait_send()


def grad_kernel(
    wide, tall, slots,
    x_ref, g_ref, a_ref, d1_ref, d3_ref, sums_ref,
    out_hbm, in_hbm, gate_hbm, up_hbm, down_hbm,
    gate, up, down, sems, o_sem,
):
    width, hidden = x_ref.shape[1], a_ref.shape[1]
    small = [
        pltpu.make_async_copy(sums_ref.at[i], dst, o_sem.at[i])
        for i, dst in enumerate((out_hbm, in_hbm))
    ]
    for copy in small:
        copy.start()

    def wide_copies(r, slot):
        span = pl.ds(pl.multiple_of(r * wide, wide), wide)
        return (
            pltpu.make_async_copy(gate.at[slot], gate_hbm.at[0, span, :], sems.at[slot, 0]),
            pltpu.make_async_copy(up.at[slot], up_hbm.at[0, span, :], sems.at[slot, 1]),
        )

    def tall_copy(r, slot):
        span = pl.ds(pl.multiple_of(r * tall, tall), tall)
        return pltpu.make_async_copy(down.at[slot], down_hbm.at[0, span, :], sems.at[slot, 2])

    steps = width // wide

    @pl.loop(0, steps)
    def _(r):
        slot = lax.rem(r, slots)

        @pl.when(r >= slots)
        def _():
            for copy in wide_copies(r - slots, slot):
                copy.wait()

        span = pl.ds(pl.multiple_of(r * wide, wide), wide)
        gate[slot] = contract_rows(x_ref[:, span], d1_ref[...]).astype(LOW)
        up[slot] = contract_rows(x_ref[:, span], d3_ref[...]).astype(LOW)
        for copy in wide_copies(r, slot):
            copy.start()

    count = hidden // tall

    @pl.loop(0, count)
    def _(r):
        slot = lax.rem(r, slots)

        @pl.when(r >= slots)
        def _():
            tall_copy(r - slots, slot).wait()

        span = pl.ds(pl.multiple_of(r * tall, tall), tall)
        down[slot] = contract_rows(a_ref[:, span], g_ref[...]).astype(LOW)
        tall_copy(r, slot).start()

    for r in range(max(0, steps - slots), steps):
        for copy in wide_copies(r, r % slots):
            copy.wait()
    for r in range(max(0, count - slots), count):
        tall_copy(r, r % slots).wait()
    for copy in small:
        copy.wait()


def per_device(tokens, cotangent, experts, gates, w_gate, w_up, w_down):
    n, m = lax.axis_size("exp"), lax.axis_size("tp")
    group = n // EXPERTS
    count, cols = tokens.shape
    width, hidden = w_gate.shape[1], w_gate.shape[2]
    rows = n * CAP
    pad = round_up(count, 16)
    bf = min(1024, hidden)
    bc = min(512, cols)

    vmem = pl.BlockSpec(memory_space=pltpu.VMEM)
    anyw = pl.BlockSpec(memory_space=pl.ANY)
    shape = jax.ShapeDtypeStruct
    dma = pltpu.SemaphoreType.DMA
    x, g, act, d1, d3, sums = pl.pallas_call(
        functools.partial(forward_kernel, n, m, group, bf, bc),
        out_shape=[shape((rows, width), LOW)] * 2
        + [shape((rows, hidden), LOW)] * 3
        + [shape((2, count, cols), LOW)],
        in_specs=[anyw, anyw, vmem, vmem, anyw, anyw, anyw],
        out_specs=[vmem] * 6,
        scratch_shapes=[
            pltpu.VMEM((width, hidden), LOW),
            pltpu.VMEM((width, hidden), LOW),
            pltpu.VMEM((hidden, width), LOW),
            dma((m, 3)),
            pltpu.VMEM((m, 2, count, cols), LOW),
            dma((2,)),
            pltpu.VMEM((128, EXPERTS * PAIR), F32),
            pltpu.VMEM((EXPERTS * PAIR, 128), LOW),
            pltpu.VMEM((4 * pad, n * PAIR), LOW),
            pltpu.VMEM((128, cols), LOW),
            pltpu.VMEM((EXPERTS, PAIR, width), LOW),
            pltpu.VMEM((n * PAIR, width), LOW),
            pltpu.VMEM((rows, hidden), F32),
            pltpu.VMEM((rows, hidden), F32),
            pltpu.VMEM((rows, hidden), F32),
            pltpu.VMEM((n * PAIR, width), LOW),
            pltpu.VMEM((n * PAIR, width), LOW),
            pltpu.VMEM((m, 2, count, cols), LOW),
            pltpu.VMEM((m, 2, count, cols), LOW),
            dma((m,)), dma((m,)), dma((m, n)), dma((m, n)),
            dma((m, n)), dma((m, n)), dma((m,)), dma((m,)),
        ],
        compiler_params=pltpu.CompilerParams(
            collective_id=0, has_side_effects=True, vmem_limit_bytes=62 * 1024 * 1024
        ),
        cost_estimate=pl.CostEstimate(
            flops=12 * rows * width * hidden,
            bytes_accessed=6 * width * hidden,
            transcendentals=rows * hidden,
        ),
        name="forward",
    )(tokens, cotangent, experts, gates, w_gate, w_up, w_down)

    wide, tall, slots = min(512, width), min(256, hidden), 3
    small = shape((count, cols), LOW)
    return pl.pallas_call(
        functools.partial(grad_kernel, wide, tall, slots),
        out_shape=[small, small]
        + [shape(w_gate.shape, LOW), shape(w_up.shape, LOW), shape(w_down.shape, LOW)],
        in_specs=[vmem] * 6,
        out_specs=[anyw] * 5,
        scratch_shapes=[
            pltpu.VMEM((slots, wide, hidden), LOW),
            pltpu.VMEM((slots, wide, hidden), LOW),
            pltpu.VMEM((slots, tall, width), LOW),
            dma((slots, 3)),
            dma((2,)),
        ],
        compiler_params=pltpu.CompilerParams(vmem_limit_bytes=48 * 1024 * 1024),
        cost_estimate=pl.CostEstimate(
            flops=6 * rows * width * hidden, bytes_accessed=6 * width * hidden, transcendentals=0
        ),
        name="grads",
    )(x, g, act, d1, d3, sums)


def solution(mesh):
    token = P("exp", "tp")
    pair = P("exp", None)
    wide = P("exp", None, "tp")
    tall = P("exp", "tp", None)
    return jax.shard_map(
        per_device,
        mesh=mesh,
        in_specs=(token, token, pair, pair, wide, wide, tall),
        out_specs=(token, token, wide, wide, tall),
        check_vma=False,
    )
```

time: 110 us -> 81.4 us (0.74)
  the two profiles are of different devices: /device:TPU:11 before, /device:TPU:0 now
where the time goes in v1:
time: 81.4 us; the launch traced here: 81 us
  Pallas kernels  71.8 us (88%)
  local copies, waits for them, and re-layouts  8.57 us (11%)
    pallas_call x1, Pallas kernels, per_device(): pl.pallas_call(functools.partial(forward_kernel, n, m, group, bf, bc), ou...  54.2 us
    pallas_call x1, Pallas kernels, per_device(): pl.pallas_call(functools.partial(grad_kernel, wide, tall, slots), out_sha...  17.6 us
    unnamed x14, local copies, waits for them, and re-layouts  8.57 us

profile of v1, /device:TPU:0, one launch (start us, length us, event | category | flops | bytes accessed | tf_op | source)
XLA Modules:
  0.0 81.0 jit_solution(17825391447842125713)
XLA Ops:
  0.6 1.4 %copy.12.experts_ref = s32[28,2]{1,0:T(8,128)} copy(s32[28,2]{0,1:T(2,128)} %param.9) | data formatting | bytes 448 | tf_op args[2]
  2.0 1.4 %copy.13.gates_ref = f32[28,2]{1,0:T(8,128)} copy(f32[28,2]{0,1:T(2,128)} %param.10) | data formatting | bytes 448 | tf_op args[3]
  3.4 54.2 %forward.1 = (bf16[64,4096]{1,0:T(8,128)(2,1)}, bf16[64,4096]{1,0:T(8,128)(2,1)}, bf16[64,2048]{1,0:T(8,128)(2,1)}, bf16[64,2048]{1,0:T(8,128)(2,1)}, bf16[64,20...) custom-call(bf16[28,1024]{1,0:T(8,128)(2,1)} %tok_hbm.1, bf16[28,1024]{1,0:T(8,128)(2,1)} %cot_hbm.1, ...), custom_call_target="tpu_custom_call" | custom-call | flops 6442450944 | bytes 50331648 | tf_op jit(solution)/shard_map/forward/pallas_call | solution.py:370
  57.6 0.0 copy-start
  57.6 1.0 %copy-done = bf16[64,4096]{1,0:T(8,128)(2,1)S(1)} copy-done((bf16[64,4096]{1,0:T(8,128)(2,1)S(1)}, bf16[64,4096]{1,0:T(8,128)(2,1)}, u32[]{:S(2)}) %copy-start) | copy-done | bytes 524312
  58.6 0.0 copy-start.1
  58.6 1.0 %copy-done.1 = bf16[64,4096]{1,0:T(8,128)(2,1)S(1)} copy-done((bf16[64,4096]{1,0:T(8,128)(2,1)S(1)}, bf16[64,4096]{1,0:T(8,128)(2,1)}, u32[]{:S(2)}) %copy-start.1) | copy-done | bytes 524312
  59.6 0.0 copy-start.2
  59.6 0.9 %copy-done.2 = bf16[64,2048]{1,0:T(8,128)(2,1)S(1)} copy-done((bf16[64,2048]{1,0:T(8,128)(2,1)S(1)}, bf16[64,2048]{1,0:T(8,128)(2,1)}, u32[]{:S(2)}) %copy-start.2) | copy-done | bytes 262168
  60.6 0.0 copy-start.3
  60.6 0.9 %copy-done.3 = bf16[64,2048]{1,0:T(8,128)(2,1)S(1)} copy-done((bf16[64,2048]{1,0:T(8,128)(2,1)S(1)}, bf16[64,2048]{1,0:T(8,128)(2,1)}, u32[]{:S(2)}) %copy-start.3) | copy-done | bytes 262168
  61.5 0.0 copy-start.4
  61.6 0.9 %copy-done.4 = bf16[64,2048]{1,0:T(8,128)(2,1)S(1)} copy-done((bf16[64,2048]{1,0:T(8,128)(2,1)S(1)}, bf16[64,2048]{1,0:T(8,128)(2,1)}, u32[]{:S(2)}) %copy-start.4) | copy-done | bytes 262168
  62.5 0.0 copy-start.5
  62.5 0.9 %copy-done.5 = bf16[2,28,1024]{2,1,0:T(8,128)(2,1)S(1)} copy-done((bf16[2,28,1024]{2,1,0:T(8,128)(2,1)S(1)}, bf16[2,28,1024]{2,1,0:T(8,128)(2,1)}, u32[]{:S(2)}) %copy-start.5) | copy-done | bytes 114712
  63.4 17.6 %grads.1 = (bf16[28,1024]{1,0:T(8,128)(2,1)}, bf16[28,1024]{1,0:T(8,128)(2,1)}, bf16[1,4096,2048]{2,1,0:T(8,128)(2,1)}, bf16[1,4096,2048]{2,1,0:T(8,128)(2,1)}, bf16[1,2048,4096]{2,1,0:T(8,128)(2,1)}) custom-call(bf16[64,4096]{1,0:T(8,128)(2,1)S(1)} %copy-done, bf16[64,4096]{1,0:T(8,128)(2,1)S(1)} %copy-done.1, bf16[64,2048]{1,0:T(8,128)(2,1)S(1)} %copy-done.2, ...), custom_call_target="tpu_custom_call" | custom-call | flops 3221225472 | bytes 50331648 | tf_op jit(solution)/shard_map/grads/pallas_call | solution.py:413
Async XLA Ops:
  57.6 1.0 %copy-start = (bf16[64,4096]{1,0:T(8,128)(2,1)S(1)}, bf16[64,4096]{1,0:T(8,128)(2,1)}, u32[]{:S(2)}) copy-start(bf16[64,4096]{1,0:T(8,128)(2,1)} %get-tuple-element.11.x_ref) | copy-start | bytes 1572868
  58.6 1.0 %copy-start.1 = (bf16[64,4096]{1,0:T(8,128)(2,1)S(1)}, bf16[64,4096]{1,0:T(8,128)(2,1)}, u32[]{:S(2)}) copy-start(bf16[64,4096]{1,0:T(8,128)(2,1)} %get-tuple-element.12.g_ref) | copy-start | bytes 1572868
  59.6 0.9 %copy-start.2 = (bf16[64,2048]{1,0:T(8,128)(2,1)S(1)}, bf16[64,2048]{1,0:T(8,128)(2,1)}, u32[]{:S(2)}) copy-start(bf16[64,2048]{1,0:T(8,128)(2,1)} %get-tuple-element.13.a_ref) | copy-start | bytes 786436
  60.6 0.9 %copy-start.3 = (bf16[64,2048]{1,0:T(8,128)(2,1)S(1)}, bf16[64,2048]{1,0:T(8,128)(2,1)}, u32[]{:S(2)}) copy-start(bf16[64,2048]{1,0:T(8,128)(2,1)} %get-tuple-element.14.d1_ref) | copy-start | bytes 786436
  61.5 0.9 %copy-start.4 = (bf16[64,2048]{1,0:T(8,128)(2,1)S(1)}, bf16[64,2048]{1,0:T(8,128)(2,1)}, u32[]{:S(2)}) copy-start(bf16[64,2048]{1,0:T(8,128)(2,1)} %get-tuple-element.15.d3_ref) | copy-start | bytes 786436
  62.5 0.9 %copy-start.5 = (bf16[2,28,1024]{2,1,0:T(8,128)(2,1)S(1)}, bf16[2,28,1024]{2,1,0:T(8,128)(2,1)}, u32[]{:S(2)}) copy-start(bf16[2,28,1024]{2,1,0:T(8,128)(2,1)} %get-tuple-element.16.sums_ref) | copy-start | bytes 344068

commit v2 on v1

v2 whole, which is shorter than its diff:
```python
import functools

import jax
import jax.numpy as jnp
from jax import lax
from jax.experimental import pallas as pl
from jax.experimental.pallas import tpu as pltpu
from jax.sharding import PartitionSpec as P

EXPERTS = 8
CAP = 8
PAIR = 2 * CAP
MESH = pl.DeviceIdType.MESH
LOW = jnp.bfloat16
F32 = jnp.float32


def contract_rows(left, right):
    return lax.dot_general(left, right, (((0,), (0,)), ((), ())), preferred_element_type=F32)


def contract_cols(left, right):
    return lax.dot_general(left, right, (((1,), (1,)), ((), ())), preferred_element_type=F32)


def flip(index, bits):
    out, unit = index, 1
    while unit <= bits:
        if bits & unit:
            out = out + unit * (1 - 2 * ((index // unit) % 2))
        unit *= 2
    return out


def round_up(value, unit):
    return -(-value // unit) * unit


def make_tables(group, count, routes, table, pick, comb):
    pad = round_up(count, 16)
    lane = lax.broadcasted_iota(jnp.int32, (count, 128), 1)
    ids = [routes[0:count, j : j + 1].astype(jnp.int32) for j in range(2)]
    gates = [routes[0:count, 8 + j : 9 + j] for j in range(2)]
    hits = [(ids[j] == lane).astype(F32) for j in range(2)]
    tri = (
        lax.broadcasted_iota(jnp.int32, (count, count), 0)
        > lax.broadcasted_iota(jnp.int32, (count, count), 1)
    ).astype(F32)
    before = jnp.dot(tri, hits[0] + hits[1], preferred_element_type=F32)
    places = [
        ids[j] * CAP + jnp.sum(before * hits[j], axis=1, keepdims=True).astype(jnp.int32)
        for j in range(2)
    ]
    table[...] = jnp.zeros_like(table)
    comb[...] = jnp.zeros_like(comb)

    def columns(width, share):
        col = lax.broadcasted_iota(jnp.int32, (count, width), 1)
        owner = col // (PAIR * share)
        return owner * CAP + col % CAP, (col % PAIR) < CAP

    where, first = columns(EXPERTS * PAIR, 1)
    hit = [places[j] == where for j in range(2)]
    table[0:count, :] = ((hit[0] | hit[1]) & first).astype(F32)
    for j in range(2):
        table[(1 + j) * pad : (1 + j) * pad + count, :] = jnp.where(first, 0.0, hit[j].astype(F32))
    pick[...] = table[...].T.astype(LOW)

    where, first = columns(comb.shape[1], group)
    hit = [(places[j] == where).astype(F32) for j in range(2)]
    weight = jnp.where(first, hit[0] * gates[0] + hit[1] * gates[1], 0.0)
    for part in range(3):
        piece = weight.astype(LOW)
        comb[part * pad : part * pad + count, :] = piece
        weight = weight - piece.astype(F32)
    comb[3 * pad : 3 * pad + count, :] = jnp.where(first, 0.0, hit[0] + hit[1]).astype(LOW)


def forward_kernel(
    n, m, group, split, bf,
    tok_hbm, cot_hbm, experts_hbm, gates_hbm, wg_hbm, wu_hbm, wd_hbm,
    x_hbm, g_hbm, a_hbm, d1_hbm, d3_hbm, out_ref,
    x_ref, g_ref, a_ref, d1_ref, d3_ref, k_sem, ids_in, gates_in, routes, wg, wu, wd, w_sem, tok, t_sem, table, pick, comb, stack, send, held,
    h1_acc, h3_acc, da_acc, back, home, part_send, got,
    sa, ra, sb, rb, rc, sd, rd,
):
    e, t = lax.axis_index("exp"), lax.axis_index("tp")
    count, cols = tok_hbm.shape
    hidden = wg.shape[1]
    pad = round_up(count, 16)
    cw = cols // split
    parts = [flip(t, q) for q in range(m)]
    low = [q & -q for q in range(m)]
    order = [0] + sorted(range(1, m), key=lambda q: (-low[q], q))

    def part_cols(q):
        return pl.ds(pl.multiple_of(parts[q] * cols, cols), cols)

    def cols_of(q, h):
        return pl.ds(pl.multiple_of(parts[q] * cols + h * cw, cw), cw)

    def rows_of(device):
        return pl.ds(pl.multiple_of(device * PAIR, PAIR), PAIR)

    own = [
        pltpu.make_async_copy(
            src.at[:, pl.ds(h * cw, cw)], tok.at[0, h, i], t_sem.at[2 + 2 * h + i]
        )
        for h in range(split)
        for i, src in enumerate((tok_hbm, cot_hbm))
    ]
    routing = [
        pltpu.make_async_copy(experts_hbm, ids_in, t_sem.at[0]),
        pltpu.make_async_copy(gates_hbm, gates_in, t_sem.at[1]),
    ]
    for copy in routing + own:
        copy.start()
    barrier = pltpu.get_barrier_semaphore()
    for r in range(1, n):
        pl.semaphore_signal(
            barrier, inc=1, device_id={"exp": lax.rem(e + r, n), "tp": t}, device_id_type=MESH
        )
    for q in range(1, m):
        pl.semaphore_signal(
            barrier, inc=1, device_id={"exp": e, "tp": parts[q]}, device_id_type=MESH
        )
    loads = {}
    for q in order:
        span = part_cols(q)
        loads[q] = (
            pltpu.make_async_copy(wg_hbm.at[0, span, :], wg.at[span, :], w_sem.at[q, 0]),
            pltpu.make_async_copy(wu_hbm.at[0, span, :], wu.at[span, :], w_sem.at[q, 1]),
            pltpu.make_async_copy(wd_hbm.at[0, :, span], wd.at[:, span], w_sem.at[q, 2]),
        )
        for copy in loads[q]:
            copy.start()
    stack[...] = jnp.zeros_like(stack)
    table[...] = jnp.zeros_like(table)
    for copy in routing:
        copy.wait()
    table[0:2, 0:count] = ids_in[...].astype(F32)
    table[8:10, 0:count] = gates_in[...]
    routes[...] = table[...].T
    make_tables(group, count, routes, table, pick, comb)
    for copy in own:
        copy.wait()
    pl.semaphore_wait(barrier, n - 1 + m - 1)

    def gather(q, h):
        return pltpu.make_async_remote_copy(
            src_ref=tok.at[q - low[q], h],
            dst_ref=tok.at[q, h],
            send_sem=sa.at[q, h],
            recv_sem=ra.at[q, h],
            device_id={"exp": e, "tp": parts[low[q]]},
            device_id_type=MESH,
        )

    def to_experts(q, h, r):
        dest = lax.rem(e + r, n)
        return pltpu.make_async_remote_copy(
            src_ref=send.at[dest // group, :, cols_of(q, h)],
            dst_ref=held.at[rows_of(e), cols_of(q, h)],
            send_sem=sb.at[0],
            recv_sem=rb.at[q, h],
            device_id={"exp": dest, "tp": t},
            device_id_type=MESH,
        )

    def to_tokens(q, h, r):
        dest = lax.rem(e + r, n)
        return pltpu.make_async_remote_copy(
            src_ref=back.at[rows_of(dest), cols_of(q, h)],
            dst_ref=home.at[rows_of(e), cols_of(q, h)],
            send_sem=sb.at[1],
            recv_sem=rc.at[q, h],
            device_id={"exp": dest, "tp": t},
            device_id_type=MESH,
        )

    def to_owner(q, h):
        return pltpu.make_async_remote_copy(
            src_ref=part_send.at[q, h],
            dst_ref=got.at[q, h],
            send_sem=sd.at[q, h],
            recv_sem=rd.at[q, h],
            device_id={"exp": e, "tp": parts[low[q]]},
            device_id_type=MESH,
        )

    def each_peer(start):
        if n <= 8:
            for r in range(1, n):
                start(r)
        else:
            pl.loop(1, n)(start)

    def all_rows(ref, span, sems):
        block = ref.at[0 : (n - 1) * PAIR, span]
        return pltpu.make_async_remote_copy(
            src_ref=block,
            dst_ref=block,
            send_sem=sems,
            recv_sem=sems,
            device_id={"exp": lax.rem(e + 1, n), "tp": t},
            device_id_type=MESH,
        )

    def forward_parts(q, h):
        for child in order[1:]:
            if child - low[child] == q:
                gather(child, h).start()

    def dispatch(q):
        for h in range(split):
            if q > 0:
                gather(q, h).wait_recv()
                forward_parts(q, h)
            stack[0:count, :] = tok[q, h, 0]
            cot = tok[q, h, 1].astype(F32)
            for j in range(2):
                stack[(1 + j) * pad : (1 + j) * pad + count, :] = (
                    cot * routes[0:count, 8 + j : 9 + j]
                ).astype(LOW)
            rows = jnp.dot(pick[...], stack[...], preferred_element_type=F32).astype(LOW)
            send[:, :, cols_of(q, h)] = rows.reshape(EXPERTS, PAIR, cw)

            each_peer(lambda r: to_experts(q, h, r).start())
            held[rows_of(e), cols_of(q, h)] = send[e // group, :, cols_of(q, h)]

    def arrive(q):
        for h in range(split):
            all_rows(held, cols_of(q, h), rb.at[q, h]).wait_recv()
        span = part_cols(q)
        pair = held[:, span].astype(F32).reshape(n, 2, CAP, cols)
        x_ref[:, span] = pair[:, 0].reshape(n * CAP, cols).astype(LOW)
        g_ref[:, span] = pair[:, 1].reshape(n * CAP, cols).astype(LOW)
        for copy in loads[q]:
            copy.wait()

    def phase_one(q, start, stop):
        span = part_cols(q)

        @pl.loop(start, stop)
        def _(j):
            units = pl.ds(pl.multiple_of(j * bf, bf), bf)
            x, g = x_ref[:, span], g_ref[:, span]
            h1 = jnp.dot(x, wg[span, units], preferred_element_type=F32)
            h3 = jnp.dot(x, wu[span, units], preferred_element_type=F32)
            da = contract_cols(g, wd[units, span])
            if q == 0:
                h1_acc[:, units] = h1
                h3_acc[:, units] = h3
                da_acc[:, units] = da
            else:
                h1_acc[:, units] += h1
                h3_acc[:, units] += h3
                da_acc[:, units] += da

    def phase_two(q, h):
        span = cols_of(q, h)
        y = jnp.dot(a_ref[...], wd[:, span], preferred_element_type=F32)
        b = contract_cols(d1_ref[...], wg[span, :]) + contract_cols(d3_ref[...], wu[span, :])
        both = jnp.concatenate([y.reshape(n, CAP, cw), b.reshape(n, CAP, cw)], axis=1)
        back[:, span] = both.reshape(n * PAIR, cw).astype(LOW)

        each_peer(lambda r: to_tokens(q, h, r).start())
        home[rows_of(e), span] = back[rows_of(e), span]

    def combine(q, h):
        all_rows(home, cols_of(q, h), rc.at[q, h]).wait_recv()
        made = jnp.dot(comb[...], home[:, cols_of(q, h)], preferred_element_type=F32)
        output = made[0:pad] + made[pad : 2 * pad] + made[2 * pad : 3 * pad]
        totals = [output[0:count], made[3 * pad : 3 * pad + count]]
        for child in range(m - 1, q, -1):
            if child - low[child] == q:
                to_owner(child, h).wait_recv()
                for i in range(2):
                    totals[i] = totals[i] + got[child, h, i].astype(F32)
        for i in range(2):
            if q > 0:
                part_send[q, h, i] = totals[i].astype(LOW)
            else:
                out_ref[i, :, h * cw : (h + 1) * cw] = totals[i].astype(LOW)
        if q > 0:
            to_owner(q, h).start()

    for h in range(split):
        forward_parts(0, h)
    chunks = hidden // bf
    middle = chunks // 2
    dispatch(order[0])
    dispatch(order[1])
    done = 0
    for i in range(2, m):
        at = order[done]
        if i % 2 == 0:
            arrive(at)
            phase_one(at, 0, middle)
        else:
            phase_one(at, middle, chunks)
            done += 1
        dispatch(order[i])
    for at in order[done:]:
        arrive(at)
        phase_one(at, 0, chunks)

    @pl.loop(0, hidden // bf)
    def _(j):
        units = pl.ds(pl.multiple_of(j * bf, bf), bf)
        h1, h3, da = h1_acc[:, units], h3_acc[:, units], da_acc[:, units]
        sig = jax.nn.sigmoid(h1)
        a_ref[:, units] = (h1 * sig * h3).astype(LOW)
        d1_ref[:, units] = (da * h3 * sig * (1.0 + h1 * (1.0 - sig))).astype(LOW)
        d3_ref[:, units] = (da * h1 * sig).astype(LOW)

    keep = [
        pltpu.make_async_copy(src, dst, k_sem.at[i])
        for i, (src, dst) in enumerate((
            (x_ref, x_hbm), (g_ref, g_hbm), (a_ref, a_hbm), (d1_ref, d1_hbm), (d3_ref, d3_hbm)
        ))
    ]
    for copy in keep:
        copy.start()

    todo = [(q, h) for q in reversed(range(m)) for h in range(split)]
    for i, (q, h) in enumerate(todo):
        phase_two(q, h)
        if i >= 2:
            combine(*todo[i - 2])
    for q, h in todo[-2:]:
        combine(q, h)

    for copy in keep:
        copy.wait()
    for q in range(m):
        for h in range(split):
            if q > 0:
                gather(q, h).wait_send()
                to_owner(q, h).wait_send()

    for i in range(2):
        all_rows(held, pl.ds(0, m * cols), sb.at[i]).wait_send()

def grad_kernel(
    wide, tall, slots,
    x_hbm, d1_hbm, d3_hbm, a_hbm, g_hbm, sums_hbm,
    out_hbm, in_hbm, gate_hbm, up_hbm, down_hbm,
    x_ref, d1_ref, d3_ref, a_ref, g_ref, sums_ref, gate, up, down, i_sem, sems, o_sem,
):
    width, hidden = x_ref.shape[1], a_ref.shape[1]
    small = [
        pltpu.make_async_copy(sums_ref.at[i], dst, o_sem.at[i])
        for i, dst in enumerate((out_hbm, in_hbm))
    ]
    loads = [
        pltpu.make_async_copy(src, dst, i_sem.at[i])
        for i, (src, dst) in enumerate((
            (x_hbm, x_ref), (d1_hbm, d1_ref), (d3_hbm, d3_ref),
            (a_hbm, a_ref), (g_hbm, g_ref), (sums_hbm, sums_ref),
        ))
    ]
    for copy in loads:
        copy.start()

    def copies(which, r, slot):
        kept, hbm, size = (
            (gate, gate_hbm, wide), (up, up_hbm, wide), (down, down_hbm, tall)
        )[which]
        span = pl.ds(pl.multiple_of(r * size, size), size)
        return pltpu.make_async_copy(kept.at[slot], hbm.at[0, span, :], sems.at[slot, which])

    def strip(which, r, left, right, kept, size):
        slot = lax.rem(r, slots)

        @pl.when(r >= slots)
        def _():
            copies(which, r - slots, slot).wait()

        span = pl.ds(pl.multiple_of(r * size, size), size)
        kept[slot] = contract_rows(left[:, span], right[...]).astype(LOW)
        copies(which, r, slot).start()

    for copy in loads[:2]:
        copy.wait()
    steps, count = width // wide, hidden // tall

    @pl.loop(0, steps)
    def _(r):
        strip(0, r, x_ref, d1_ref, gate, wide)

    for copy in loads[2:]:
        copy.wait()
    for copy in small:
        copy.start()

    @pl.loop(0, steps)
    def _(r):
        strip(1, r, x_ref, d3_ref, up, wide)

    @pl.loop(0, count)
    def _(r):
        strip(2, r, a_ref, g_ref, down, tall)

    for which, total in ((0, steps), (1, steps), (2, count)):
        for r in range(max(0, total - slots), total):
            copies(which, r, r % slots).wait()
    for copy in small:
        copy.wait()


def per_device(tokens, cotangent, experts, gates, w_gate, w_up, w_down):
    n, m = lax.axis_size("exp"), lax.axis_size("tp")
    group = n // EXPERTS
    count, cols = tokens.shape
    width, hidden = w_gate.shape[1], w_gate.shape[2]
    rows = n * CAP
    pad = round_up(count, 16)
    bf = min(1024, hidden)
    split = 2

    vmem = pl.BlockSpec(memory_space=pltpu.VMEM)
    anyw = pl.BlockSpec(memory_space=pl.ANY)
    shape = jax.ShapeDtypeStruct
    dma = pltpu.SemaphoreType.DMA
    x, g, act, d1, d3, sums = pl.pallas_call(
        functools.partial(forward_kernel, n, m, group, split, bf),
        out_shape=[shape((rows, width), LOW)] * 2
        + [shape((rows, hidden), LOW)] * 3
        + [shape((2, count, cols), LOW)],
        in_specs=[anyw] * 7,
        out_specs=[anyw] * 5 + [vmem],
        scratch_shapes=[
            pltpu.VMEM((rows, width), LOW),
            pltpu.VMEM((rows, width), LOW),
            pltpu.VMEM((rows, hidden), LOW),
            pltpu.VMEM((rows, hidden), LOW),
            pltpu.VMEM((rows, hidden), LOW),
            dma((5,)),
            pltpu.VMEM((2, count), jnp.int32),
            pltpu.VMEM((2, count), F32),
            pltpu.VMEM((128, 128), F32),
            pltpu.VMEM((width, hidden), LOW),
            pltpu.VMEM((width, hidden), LOW),
            pltpu.VMEM((hidden, width), LOW),
            dma((m, 3)),
            pltpu.VMEM((m, split, 2, count, cols // split), LOW),
            dma((2 + 2 * split,)),
            pltpu.VMEM((128, EXPERTS * PAIR), F32),
            pltpu.VMEM((EXPERTS * PAIR, 128), LOW),
            pltpu.VMEM((4 * pad, n * PAIR), LOW),
            pltpu.VMEM((128, cols // split), LOW),
            pltpu.VMEM((EXPERTS, PAIR, width), LOW),
            pltpu.VMEM((n * PAIR, width), LOW),
            pltpu.VMEM((rows, hidden), F32),
            pltpu.VMEM((rows, hidden), F32),
            pltpu.VMEM((rows, hidden), F32),
            pltpu.VMEM((n * PAIR, width), LOW),
            pltpu.VMEM((n * PAIR, width), LOW),
            pltpu.VMEM((m, split, 2, count, cols // split), LOW),
            pltpu.VMEM((m, split, 2, count, cols // split), LOW),
            dma((m, split)), dma((m, split)), dma((2,)), dma((m, split)),
            dma((m, split)), dma((m, split)), dma((m, split)),
        ],
        compiler_params=pltpu.CompilerParams(
            collective_id=0, has_side_effects=True, vmem_limit_bytes=62 * 1024 * 1024
        ),
        cost_estimate=pl.CostEstimate(
            flops=12 * rows * width * hidden,
            bytes_accessed=6 * width * hidden,
            transcendentals=rows * hidden,
        ),
        name="forward",
    )(tokens, cotangent, experts.T, gates.T, w_gate, w_up, w_down)

    wide, tall, slots = min(1024, width), min(512, hidden), 3
    small = shape((count, cols), LOW)
    return pl.pallas_call(
        functools.partial(grad_kernel, wide, tall, slots),
        out_shape=[small, small]
        + [shape(w_gate.shape, LOW), shape(w_up.shape, LOW), shape(w_down.shape, LOW)],
        in_specs=[anyw] * 6,
        out_specs=[anyw] * 5,
        scratch_shapes=[
            pltpu.VMEM((rows, width), LOW),
            pltpu.VMEM((rows, hidden), LOW),
            pltpu.VMEM((rows, hidden), LOW),
            pltpu.VMEM((rows, hidden), LOW),
            pltpu.VMEM((rows, width), LOW),
            pltpu.VMEM((2, count, cols), LOW),
            pltpu.VMEM((slots, wide, hidden), LOW),
            pltpu.VMEM((slots, wide, hidden), LOW),
            pltpu.VMEM((slots, tall, width), LOW),
            dma((6,)),
            dma((slots, 3)),
            dma((2,)),
        ],
        compiler_params=pltpu.CompilerParams(vmem_limit_bytes=62 * 1024 * 1024),
        cost_estimate=pl.CostEstimate(
            flops=6 * rows * width * hidden, bytes_accessed=6 * width * hidden, transcendentals=0
        ),
        name="grads",
    )(x, d1, d3, act, g, sums)


def solution(mesh):
    token = P("exp", "tp")
    pair = P("exp", None)
    wide = P("exp", None, "tp")
    tall = P("exp", "tp", None)
    return jax.shard_map(
        per_device,
        mesh=mesh,
        in_specs=(token, token, pair, pair, wide, wide, tall),
        out_specs=(token, token, wide, wide, tall),
        check_vma=False,
    )
```

time: 81.4 us -> 67.7 us (0.83)
  local copies, waits for them, and re-layouts: 8.57 us -> 0 us
  Pallas kernels: 71.8 us -> 66.8 us
    unnamed x14 -> x0, local copies, waits for them, and re-layouts: 8.57 us -> none
    pallas_call x1, Pallas kernels: 54.2 us -> 48 us  [per_device(): pl.pallas_call(functools.partial(forward_kernel, n, m, group, split, bf),...]
    pallas_call x1, Pallas kernels: 17.6 us -> 18.7 us  [per_device(): pl.pallas_call(functools.partial(grad_kernel, wide, tall, slots), out_sha...]
where the time goes in v2:
time: 67.7 us; the launch traced here: 67.6 us
  Pallas kernels  66.8 us (99%)
  between operations  0.82 us (1%)
    pallas_call x1, Pallas kernels, per_device(): pl.pallas_call(functools.partial(forward_kernel, n, m, group, split, bf),...  48 us
    pallas_call x1, Pallas kernels, per_device(): pl.pallas_call(functools.partial(grad_kernel, wide, tall, slots), out_sha...  18.7 us

profile of v2, /device:TPU:0, one launch (start us, length us, event | category | flops | bytes accessed | tf_op | source)
XLA Modules:
  0.0 67.6 jit_solution(10480806455512901454)
XLA Ops:
  0.6 48.0 %forward.1 = (bf16[64,4096]{1,0:T(8,128)(2,1)}, bf16[64,4096]{1,0:T(8,128)(2,1)}, bf16[64,2048]{1,0:T(8,128)(2,1)}, bf16[64,2048]{1,0:T(8,128)(2,1)}, bf16[64,20...) custom-call(bf16[28,1024]{1,0:T(8,128)(2,1)} %tok_hbm.1, bf16[28,1024]{1,0:T(8,128)(2,1)} %cot_hbm.1, s32[2,28]{1,0:T(2,128)} %bitcast.2, ...), custom_call_target="tpu_custom_call" | custom-call | flops 6442450944 | bytes 50331648 | tf_op jit(solution)/shard_map/forward/pallas_call | solution.py:426
  48.7 18.7 %grads.1 = (bf16[28,1024]{1,0:T(8,128)(2,1)}, bf16[28,1024]{1,0:T(8,128)(2,1)}, bf16[1,4096,2048]{2,1,0:T(8,128)(2,1)}, bf16[1,4096,2048]{2,1,0:T(8,128)(2,1)}, bf16[1,2048,4096]{2,1,0:T(8,128)(2,1)}) custom-call(bf16[64,4096]{1,0:T(8,128)(2,1)} %get-tuple-element.11.x_hbm, bf16[64,2048]{1,0:T(8,128)(2,1)} %get-tuple-element.12.d1_hbm, ...), custom_call_target="tpu_custom_call" | custom-call | flops 3221225472 | bytes 50331648 | tf_op jit(solution)/shard_map/grads/pallas_call | solution.py:478

commit v3 on v2

--- a/solution.py
+++ b/solution.py
@@ -206,16 +206,17 @@
             device_id_type=MESH,
         )
 
-    def forward_parts(q, h):
+    def forward_parts(q, halves):
         for child in order[1:]:
             if child - low[child] == q:
-                gather(child, h).start()
+                for h in halves:
+                    gather(child, h).start()
 
     def dispatch(q):
         for h in range(split):
             if q > 0:
                 gather(q, h).wait_recv()
-                forward_parts(q, h)
+                forward_parts(q, [h])
             stack[0:count, :] = tok[q, h, 0]
             cot = tok[q, h, 1].astype(F32)
             for j in range(2):
@@ -285,8 +286,7 @@
         if q > 0:
             to_owner(q, h).start()
 
-    for h in range(split):
-        forward_parts(0, h)
+    forward_parts(0, range(split))
     chunks = hidden // bf
     middle = chunks // 2
     dispatch(order[0])
@@ -416,7 +416,7 @@
     width, hidden = w_gate.shape[1], w_gate.shape[2]
     rows = n * CAP
     pad = round_up(count, 16)
-    bf = min(1024, hidden)
+    bf = min(2048, hidden)
     split = 2
 
     vmem = pl.BlockSpec(memory_space=pltpu.VMEM)

time: 67.7 us -> 66.6 us (0.984)
  Pallas kernels: 66.8 us -> 65.7 us
    pallas_call x1, Pallas kernels: 48 us -> 47 us  [per_device(): pl.pallas_call(functools.partial(forward_kernel, n, m, group, split, bf),...]
where the time goes in v3:
time: 66.6 us; the launch traced here: 66.5 us
  Pallas kernels  65.7 us (99%)
  between operations  0.8 us (1%)
    pallas_call x1, Pallas kernels, per_device(): pl.pallas_call(functools.partial(forward_kernel, n, m, group, split, bf),...  47 us
    pallas_call x1, Pallas kernels, per_device(): pl.pallas_call(functools.partial(grad_kernel, wide, tall, slots), out_sha...  18.7 us

profile of v3, /device:TPU:0, one launch (start us, length us, event | category | flops | bytes accessed | tf_op | source)
XLA Modules:
  0.0 66.5 jit_solution(7566047198666586282)
XLA Ops:
  0.6 47.0 %forward.1 = (bf16[64,4096]{1,0:T(8,128)(2,1)}, bf16[64,4096]{1,0:T(8,128)(2,1)}, bf16[64,2048]{1,0:T(8,128)(2,1)}, bf16[64,2048]{1,0:T(8,128)(2,1)}, bf16[64,20...) custom-call(bf16[28,1024]{1,0:T(8,128)(2,1)} %tok_hbm.1, bf16[28,1024]{1,0:T(8,128)(2,1)} %cot_hbm.1, s32[2,28]{1,0:T(2,128)} %bitcast.2, ...), custom_call_target="tpu_custom_call" | custom-call | flops 6442450944 | bytes 50331648 | tf_op jit(solution)/shard_map/forward/pallas_call | solution.py:426
  47.6 18.7 %grads.1 = (bf16[28,1024]{1,0:T(8,128)(2,1)}, bf16[28,1024]{1,0:T(8,128)(2,1)}, bf16[1,4096,2048]{2,1,0:T(8,128)(2,1)}, bf16[1,4096,2048]{2,1,0:T(8,128)(2,1)}, bf16[1,2048,4096]{2,1,0:T(8,128)(2,1)}) custom-call(bf16[64,4096]{1,0:T(8,128)(2,1)} %get-tuple-element.11.x_hbm, bf16[64,2048]{1,0:T(8,128)(2,1)} %get-tuple-element.12.d1_hbm, ...), custom_call_target="tpu_custom_call" | custom-call | flops 3221225472 | bytes 50331648 | tf_op jit(solution)/shard_map/grads/pallas_call | solution.py:478
